TPU v7x, 8 devices: a whole 2x2x1 slice. The times are simulated.
8 devices in a mesh: dp: 1 (over z), tp: 8 (over y, x, core).
Axes of the slice: x: 2, y: 2, z: 1, core: 2. Of those that a mesh axis runs over, the one named last changes fastest.
Arguments:
- hidden: bfloat16 [128, 1, 1536], P('dp')
- ln_gain: bfloat16 [2, 2, 1536], replicated
- ln_shift: bfloat16 [2, 2, 1536], replicated
- w_qkv: bfloat16 [2, 1536, 4608], P(None, None, 'tp')
- b_qkv: bfloat16 [2, 4608], P(None, 'tp')
- w_out: bfloat16 [2, 1536, 1536], P(None, 'tp')
- b_out: bfloat16 [2, 1536], replicated
- w_up: bfloat16 [2, 1536, 6144], P(None, None, 'tp')
- b_up: bfloat16 [2, 6144], P(None, 'tp')
- w_down: bfloat16 [2, 6144, 1536], P(None, 'tp')
- b_down: bfloat16 [2, 1536], replicated
- k_cache: bfloat16 [2, 128, 256, 16, 96], P(None, 'dp', None, 'tp')
- v_cache: bfloat16 [2, 128, 256, 16, 96], P(None, 'dp', None, 'tp')
- write_slot: int32 [128], P('dp')
- key_pos: int32 [128, 256], P('dp')
- key_valid: int32 [128, 256], P('dp')
Outputs:
- output 1: bfloat16 [128, 1, 1536], P('dp')
- output 2: bfloat16 [2, 128, 256, 16, 96], P(None, 'dp', None, 'tp')
- output 3: bfloat16 [2, 128, 256, 16, 96], P(None, 'dp', None, 'tp')
All inputs are finite; a program needn't handle non-finite values.
Results may differ from a plain program's by a relative error of at most 0.0130407.
Values are sent between devices in bfloat16 or wider.
A program may use at most 1 GiB of HBM per device.

v0:
```python
import math
import jax
import jax.numpy as jnp
from jax import lax
from jax.sharding import PartitionSpec as P

LN_EPS = 1e-5


def alibi_slopes(n_heads):
    return jnp.exp2(-8.0 * jnp.arange(1, n_heads + 1).astype(jnp.float32) / n_heads)


def layer_norm(x_rows, gain, shift):
    x_f32 = x_rows.astype(jnp.float32)
    mean_val = jnp.mean(x_f32, axis=-1, keepdims=True)
    centered = x_f32 - mean_val
    var_val = jnp.mean(centered * centered, axis=-1, keepdims=True)
    normed = centered * lax.rsqrt(var_val + LN_EPS)
    return (normed * gain.astype(jnp.float32) + shift.astype(jnp.float32)).astype(jnp.bfloat16)


def solution(mesh):
    tp_size = mesh.shape['tp']

    def device_step(hidden, ln_gain, ln_shift, w_qkv, b_qkv, w_out, b_out, w_up, b_up, w_down, b_down, k_cache, v_cache, write_slot, key_pos, key_valid):
        n_layers, n_batch, cache_len, n_local, head_dim = k_cache.shape
        all_slopes = alibi_slopes(n_local * tp_size)
        my_slopes = lax.dynamic_slice_in_dim(all_slopes, lax.axis_index('tp') * n_local, n_local)
        t_index = lax.broadcasted_iota(jnp.int32, (n_batch, cache_len), 1)
        is_new = t_index == write_slot[:, None]
        allowed = jnp.logical_or(key_valid > 0, is_new)
        pos_bias = jnp.where(allowed[:, None, :], my_slopes[None, :, None] * key_pos.astype(jnp.float32)[:, None, :], -jnp.inf)
        new_mask = is_new[:, :, None, None]
        score_scale = 1.0 / math.sqrt(head_dim)
        x_cur = hidden[:, 0, :]
        k_list = []
        v_list = []
        for layer_idx in range(n_layers):
            normed = layer_norm(x_cur, ln_gain[layer_idx, 0], ln_shift[layer_idx, 0])
            qkv_out = (jnp.dot(normed, w_qkv[layer_idx], preferred_element_type=jnp.float32) + b_qkv[layer_idx].astype(jnp.float32)).astype(jnp.bfloat16)
            qkv_out = qkv_out.reshape(n_batch, n_local, 3, head_dim)
            k_all = jnp.where(new_mask, qkv_out[:, None, :, 1, :], k_cache[layer_idx])
            v_all = jnp.where(new_mask, qkv_out[:, None, :, 2, :], v_cache[layer_idx])
            scores = jnp.einsum('bhd,bthd->bht', qkv_out[:, :, 0, :], k_all, preferred_element_type=jnp.float32) * score_scale + pos_bias
            attn_probs = jax.nn.softmax(scores, axis=-1).astype(jnp.bfloat16)
            attn_out = jnp.einsum('bht,bthd->bhd', attn_probs, v_all, preferred_element_type=jnp.float32).astype(jnp.bfloat16)
            proj_part = jnp.dot(attn_out.reshape(n_batch, n_local * head_dim), w_out[layer_idx], preferred_element_type=jnp.float32)
            proj_sum = lax.psum(proj_part, 'tp')
            x_mid = (x_cur.astype(jnp.float32) + proj_sum + b_out[layer_idx].astype(jnp.float32)).astype(jnp.bfloat16)
            normed_mlp = layer_norm(x_mid, ln_gain[layer_idx, 1], ln_shift[layer_idx, 1])
            up_act = jnp.dot(normed_mlp, w_up[layer_idx], preferred_element_type=jnp.float32) + b_up[layer_idx].astype(jnp.float32)
            gelu_out = jax.nn.gelu(up_act, approximate=True).astype(jnp.bfloat16)
            down_part = jnp.dot(gelu_out, w_down[layer_idx], preferred_element_type=jnp.float32)
            down_sum = lax.psum(down_part, 'tp')
            x_cur = (x_mid.astype(jnp.float32) + down_sum + b_down[layer_idx].astype(jnp.float32)).astype(jnp.bfloat16)
            k_list.append(k_all)
            v_list.append(v_all)
        return x_cur[:, None, :], jnp.stack(k_list), jnp.stack(v_list)

    cache_spec = P(None, 'dp', None, 'tp', None)
    in_specs = (P('dp', None, None), P(), P(), P(None, None, 'tp'), P(None, 'tp'), P(None, 'tp', None), P(), P(None, None, 'tp'), P(None, 'tp'), P(None, 'tp', None), P(), cache_spec, cache_spec, P('dp'), P('dp', None), P('dp', None))
    out_specs = (P('dp', None, None), cache_spec, cache_spec)
    return jax.shard_map(device_step, mesh=mesh, in_specs=in_specs, out_specs=out_specs, check_vma=False)
```

profile of v0, /device:TPU:0, one launch (start us, length us, event | category | flops | bytes accessed | tf_op | source)
XLA Modules:
  0.0 283.8 jit_solution(13370903894764914069)
XLA Ops:
  7.2 1.1 convert_reduce_fusion.3
  8.4 1.2 fusion.87
  9.6 0.8 convert_reduce_fusion.18
  10.4 0.9 convert_element_type.183
  11.3 0.9 convert_reduce_fusion.5
  12.3 2.3 fusion.59
  15.1 1.0 compare_or_fusion
  16.1 7.0 %fusion.7 = f32[128,2,1,256]{3,2,1,0:T(1,128)S(1)} fusion(bf16[128,2,96,1]{2,3,1,0:T(2,128)(2,1)S(1)} %copy.43, pred[128,256]{1,0:T(8,128)(4,1)S(1)} %get-tuple-element.38, bf16[2,128,256,2,96]{2,4,3,1,0:T(8,128)(2,1)} %param.27, bf16[128,2,96]{2,1,0:T(2,128)(2,1)S(1)} %copy.35), kind=kOutput, calls=%fused_computation.13 | convolution fusion | flops 18874368 | bytes 12976128 | tf_op jit(solution)/shard_map/bhd,bthd->bht/dot_general | solution.py:45
  23.1 0.3 fusion.64
  23.5 7.1 %fusion.6 = bf16[128,2,1,96]{3,2,1,0:T(2,128)(2,1)S(1)} fusion(pred[128,256]{1,0:T(8,128)(4,1)S(1)} %get-tuple-element.38, bf16[2,128,256,2,96]{2,4,3,1,0:T(8,128)(2,1)} %param.28, bf16[128,2,96]{2,1,0:T(2,128)(2,1)S(1)} %copy.36, bf16[128,2,256,1]{2,0,1,3:T(8,128)(2,1)S(1)} %fusion.64), kind=kOutput, calls=%fused_computation.11 | convolution fusion | flops 18874368 | bytes 12845056 | tf_op jit(solution)/shard_map/bht,bthd->bhd/dot_general | solution.py:47
  30.7 1.2 fusion.102
  32.1 46.9 %all-reduce.5.cloned.1.call-done = f32[128,1536]{1,0:T(8,128)} async-done(((f32[128,1536]{1,0:T(8,128)}), f32[128,1536]{1,0:T(8,128)}) %all-reduce.5.cloned.1.call-update) | async-done | bytes 786448 | tf_op jit(solution)/shard_map/psum | solution.py:49
  79.0 1.3 convert_reduce_fusion.2
  80.3 0.3 fusion.82
  80.6 4.4 %fusion.24 = f32[128,1536]{1,0:T(8,128)} fusion(bf16[2,768,1536]{2,1,0:T(8,128)(2,1)} %param.25, bf16[2,1536,768]{2,1,0:T(8,128)(2,1)} %param.23, bf16[128,1536]{1,0:T(8,128)(2,1)S(1)} %get-tuple-element.24, f32[1536]{0:T(1024)S(1)} %get-tuple-element.8, f32[1536]{0:T(1024)S(1)} %get-tuple-element.41, f32[128]{0:T(128)S(1)} %add_rsqrt_fusion.2, ...), kind=kOutput, calls=%fused_computation.34 | convolution fusion | flops 606142464 | bytes 5914624 | tf_op jit(solution)/shard_map/dot_general | solution.py:54
  85.1 43.4 %all-reduce.7.cloned.1.call-done = f32[128,1536]{1,0:T(8,128)} async-done(((f32[128,1536]{1,0:T(8,128)}), f32[128,1536]{1,0:T(8,128)}) %all-reduce.7.cloned.1.call-update) | async-done | bytes 786448 | tf_op jit(solution)/shard_map/psum | solution.py:55
  128.6 1.3 convert_reduce_fusion.1
  129.9 0.3 fusion.78
  130.2 2.2 fusion.56
  132.8 7.0 %fusion.5 = f32[128,2,1,256]{3,2,1,0:T(1,128)S(1)} fusion(bf16[128,2,96,1]{2,3,1,0:T(2,128)(2,1)S(1)} %copy.47, pred[128,256]{1,0:T(8,128)(4,1)S(1)} %get-tuple-element.38, bf16[2,128,256,2,96]{2,4,3,1,0:T(8,128)(2,1)} %param.27, bf16[128,2,96]{2,1,0:T(2,128)(2,1)S(1)} %copy.37), kind=kOutput, calls=%fused_computation.9 | convolution fusion | flops 18874368 | bytes 12976128 | tf_op jit(solution)/shard_map/bhd,bthd->bht/dot_general | solution.py:45
  139.8 0.3 fusion.65
  140.1 33.7 %broadcast_select_fusion.1 = (bf16[1,128,256,2,96]{2,4,3,1,0:T(8,128)(2,1)}, bf16[1,128,256,2,96]{2,4,3,1,0:T(8,128)(2,1)}, bf16[1,128,256,2,96]{2,4,3,1,0:T(8,128)(2,1)}, bf16[1,128,256,2,96]{2,4,3,1,0:T(8,128)(2,1)}) fusion(pred[128,256]{1,0:T(8,128)(4,1)S(1)} %get-tuple-element.38, bf16[2,128,256,2,96]{2,4,3,1,0:T(8,128)(2,1)} %param.28, ...), kind=kLoop, calls=%fused_computation.15 | loop fusion | flops 25165824 | bytes 100892672 | tf_op jit(solution)/shard_map/jit(_where)/select_n | solution.py:44
  173.8 7.0 %fusion.4 = bf16[128,2,1,96]{3,2,1,0:T(2,128)(2,1)S(1)} fusion(pred[128,256]{1,0:T(8,128)(4,1)S(1)} %get-tuple-element.38, bf16[2,128,256,2,96]{2,4,3,1,0:T(8,128)(2,1)} %param.28, bf16[128,2,96]{2,1,0:T(2,128)(2,1)S(1)} %copy.38, bf16[128,2,256,1]{2,0,1,3:T(8,128)(2,1)S(1)} %fusion.65), kind=kOutput, calls=%fused_computation.7 | convolution fusion | flops 18874368 | bytes 12845056 | tf_op jit(solution)/shard_map/bht,bthd->bhd/dot_general | solution.py:47
  181.0 1.2 fusion.100
  182.2 20.6 %pad_maximum_fusion.1 = bf16[2,128,256,2,96]{2,4,3,1,0:T(8,128)(2,1)} fusion(bf16[1,128,256,2,96]{2,4,3,1,0:T(8,128)(2,1)} %get-tuple-element.26, bf16[1,128,256,2,96]{2,4,3,1,0:T(8,128)(2,1)} %get-tuple-element.25), kind=kLoop, calls=%fused_computation.5 | loop fusion | flops 12582912 | bytes 50331648 | tf_op jit(solution)/shard_map/stack | solution.py:59
  202.9 22.9 %all-reduce.9.cloned.1.call-done = f32[128,1536]{1,0:T(8,128)} async-done(((f32[128,1536]{1,0:T(8,128)}), f32[128,1536]{1,0:T(8,128)}) %all-reduce.9.cloned.1.call-update) | async-done | bytes 786448 | tf_op jit(solution)/shard_map/psum | solution.py:49
  225.7 1.3 convert_reduce_fusion
  227.1 0.3 fusion.74
  227.4 4.4 %fusion.20 = f32[128,1536]{1,0:T(8,128)} fusion(bf16[2,768,1536]{2,1,0:T(8,128)(2,1)} %param.25, bf16[2,1536,768]{2,1,0:T(8,128)(2,1)} %param.23, bf16[128,1536]{1,0:T(8,128)(2,1)S(1)} %get-tuple-element.20, f32[1536]{0:T(1024)S(1)} %get-tuple-element.7, f32[1536]{0:T(1024)S(1)} %get-tuple-element.42, f32[128]{0:T(128)S(1)} %add_rsqrt_fusion, ...), kind=kOutput, calls=%fused_computation.30 | convolution fusion | flops 606142464 | bytes 5914624 | tf_op jit(solution)/shard_map/dot_general | solution.py:54
  231.8 20.6 %pad_maximum_fusion = bf16[2,128,256,2,96]{2,4,3,1,0:T(8,128)(2,1)} fusion(bf16[1,128,256,2,96]{2,4,3,1,0:T(8,128)(2,1)} %get-tuple-element.35, bf16[1,128,256,2,96]{2,4,3,1,0:T(8,128)(2,1)} %get-tuple-element.36), kind=kLoop, calls=%fused_computation.4 | loop fusion | flops 12582912 | bytes 50331648 | tf_op jit(solution)/shard_map/stack | solution.py:59
  252.4 22.9 %all-reduce.11.cloned.1.call-done = f32[128,1536]{1,0:T(8,128)} async-done(((f32[128,1536]{1,0:T(8,128)}), f32[128,1536]{1,0:T(8,128)}) %all-reduce.11.cloned.1.call-update) | async-done | bytes 786448 | tf_op jit(solution)/shard_map/psum | solution.py:55
  275.3 2.0 fusion.134
  (41 shorter events, 1.5 us)
Async XLA Ops:
  7.2 71.8 %all-reduce.5.cloned.1.call-start = ((), (), s32[]{:S(2)}) async-start(), calls=%async_computation | async-start | bytes 1572864 | tf_op jit(solution)/shard_map/psum | solution.py:49
  23.4 7.3 %copy-start.1 = (bf16[2,192,1536]{2,1,0:T(8,128)(2,1)S(1)}, bf16[2,192,1536]{2,1,0:T(8,128)(2,1)}, u32[]{:S(2)}) copy-start(bf16[2,192,1536]{2,1,0:T(8,128)(2,1)} %param.21) | copy-start | bytes 3538948
  23.4 8.5 %copy-start.4 = (bf16[2,768]{1,0:T(2,128)(2,1)S(1)}, bf16[2,768]{1,0:T(2,128)(2,1)}, u32[]{:S(2)}) copy-start(bf16[2,768]{1,0:T(2,128)(2,1)} %param.24) | copy-start | bytes 9220
  23.5 8.6 %copy-start.2 = (bf16[2,1536]{1,0:T(2,128)(2,1)S(1)}, bf16[2,1536]{1,0:T(2,128)(2,1)}, u32[]{:S(2)}) copy-start(bf16[2,1536]{1,0:T(2,128)(2,1)} %param.22) | copy-start | bytes 18436
  23.5 55.5 %copy-start = (bf16[128,1,1536]{2,0,1:T(8,128)(2,1)S(1)}, bf16[128,1,1536]{2,0,1:T(8,128)(2,1)}, u32[]{:S(2)}) copy-start(bf16[128,1,1536]{2,0,1:T(8,128)(2,1)} %param.16) | copy-start | bytes 1179652
  30.6 54.5 %copy-start.3 = (bf16[2,1536]{1,0:T(2,128)(2,1)S(1)}, bf16[2,1536]{1,0:T(2,128)(2,1)}, u32[]{:S(2)}) copy-start(bf16[2,1536]{1,0:T(2,128)(2,1)} %param.26) | copy-start | bytes 18436
  31.9 96.6 %all-reduce.7.cloned.1.call-start = ((), (), s32[]{:S(2)}) async-start(), calls=%async_computation.1 | async-start | bytes 1572864 | tf_op jit(solution)/shard_map/psum | solution.py:55
  85.0 140.7 %all-reduce.9.cloned.1.call-start = ((), (), s32[]{:S(2)}) async-start(), calls=%async_computation.2 | async-start | bytes 1572864 | tf_op jit(solution)/shard_map/psum | solution.py:49
  182.2 93.1 %all-reduce.11.cloned.1.call-start = ((), (), s32[]{:S(2)}) async-start(), calls=%async_computation.3 | async-start | bytes 1572864 | tf_op jit(solution)/shard_map/psum | solution.py:55
Sparse Core Ops, SparseCore 0:
  32.1 46.8 all-reduce.4
  85.1 43.3 all-reduce.6
  182.3 43.3 all-reduce.8
  231.9 43.3 all-reduce.10
where the time goes:
time: 285 us; the launch traced here: 284 us
  waiting for transfers between devices  136 us (48%)
  other arithmetic  88.5 us (31%)
  matrix products  43.8 us (15%)
  between operations  14 us (5%)
    psum x2, waiting for transfers between devices, device_step(): proj_sum = lax.psum(proj_part, 'tp')  69.8 us
    psum x2, waiting for transfers between devices, device_step(): down_sum = lax.psum(down_part, 'tp')  66.4 us
    another operation x2, other arithmetic, device_step(): return (x_cur[:, None, :], jnp.stack(k_list), jnp.stack(v_list))  41.3 us
    select_n x1, other arithmetic, device_step(): v_all = jnp.where(new_mask, qkv_out[:, None, :, 2, :], v_cache[layer_idx])  33.7 us
    dot_general x2, matrix products, device_step(): jnp.einsum('bht,bthd->bhd', attn_probs, v_all, preferred_element_type=jnp...  14.1 us
    dot_general x2, matrix products, device_step(): jnp.einsum('bhd,bthd->bht', qkv_out[:, :, 0, :], k_all, preferred_element...  14 us
    dot_general x2, matrix products, device_step(): jnp.dot(gelu_out, w_down[layer_idx], preferred_element_type=jnp.float32)  8.78 us
  transfers between devices with their start and end apart: 4, of which 4 were waited for; matrix products, arithmetic and copies ran while one was open for 15% of the time, Pallas kernels for 0%

commit v1 on v0

v1 whole, which is shorter than its diff:
```python
import functools
import math

import jax
import jax.numpy as jnp
from jax import lax
from jax.experimental import pallas as pl
from jax.experimental.pallas import tpu as pltpu
from jax.sharding import PartitionSpec as P

MESH = pl.DeviceIdType.MESH
F32 = jnp.float32
BF16 = jnp.bfloat16
LN_EPS = 1e-5
BATCH, CACHE, HIDDEN, HEADS, HEAD, FFN = 128, 256, 1536, 16, 96, 6144
TP = 8
LOCAL_HEADS = HEADS // TP
HD = LOCAL_HEADS * HEAD
QKV = 3 * HD
FF = FFN // TP
GROUP = 8
NGROUP = BATCH // GROUP
GROWS = GROUP * LOCAL_HEADS
GK = GROUP * HD
ROWS = BATCH // TP
NCHUNK = 3
CHUNK = HIDDEN // NCHUNK
NT = (((1,), (1,)), ((), ()))


def dot(a, b):
    return jnp.dot(a, b, preferred_element_type=F32)


def dot_nt(a, b):
    return lax.dot_general(a, b, NT, preferred_element_type=F32)


def iota(shape, dim):
    return lax.broadcasted_iota(jnp.int32, shape, dim)


def one_hot(cond):
    return jnp.where(cond, 1.0, 0.0).astype(BF16)


def layer_norm(x, gain, shift):
    mean = jnp.mean(x, axis=-1, keepdims=True)
    centered = x - mean
    var = jnp.mean(centered * centered, axis=-1, keepdims=True)
    normed = centered * lax.rsqrt(var + LN_EPS)
    return (normed * gain.astype(F32) + shift.astype(F32)).astype(BF16)


def att_kernel(layer, *refs):
    if layer == 0:
        (x_ref, lng, lnb, wq_hbm, bq, wo_hbm, k_hbm, v_hbm, ws_ref, kp_ref, kv_ref,
         part_ref, k_out, v_out, bias_ref, new_ref,
         kbuf, vbuf, wq, wo, abuf, qbig, kvt, ebuf, sbuf, pbuf, ksem, vsem, wsem) = refs
    else:
        (x_ref, wq_hbm, bq, wo_hbm, k_hbm, v_hbm, bias_ref, new_ref, _, _,
         part_ref, k_out, v_out,
         kbuf, vbuf, wq, wo, abuf, qbig, kvt, ebuf, sbuf, pbuf, ksem, vsem, wsem) = refs
    wq_copy = pltpu.make_async_copy(wq_hbm.at[layer], wq, wsem.at[0])
    wq_copy.start()

    def k_in(g):
        return pltpu.make_async_copy(k_hbm.at[layer, g], kbuf.at[g], ksem.at[0, g])

    def v_in(g):
        return pltpu.make_async_copy(v_hbm.at[layer, g], vbuf.at[g], vsem.at[0, g])

    def k_back(g):
        return pltpu.make_async_copy(kbuf.at[g], k_out.at[layer, g], ksem.at[1, g])

    def v_back(g):
        return pltpu.make_async_copy(vbuf.at[g], v_out.at[layer, g], vsem.at[1, g])

    def start_in(g, c):
        k_in(g).start()
        v_in(g).start()
        return c

    lax.fori_loop(0, NGROUP, start_in, 0)
    wo_copies = [pltpu.make_async_copy(wo_hbm.at[layer], wo.at[pl.ds(i * HD, HD)], wsem.at[1 + i]) for i in range(2)]
    for copy in wo_copies:
        copy.start()

    expand = one_hot(iota((2 * BATCH, BATCH), 0) // 2 == iota((2 * BATCH, BATCH), 1))
    if layer == 0:
        def norm_rows(i, c):
            r = pl.ds(pl.multiple_of(i * 16, 16), 16)
            abuf[r, :] = layer_norm(x_ref[r, :].astype(F32), lng[0, 0:1, :], lnb[0, 0:1, :])
            return c

        lax.fori_loop(0, BATCH // 16, norm_rows, 0)
        me = lax.axis_index("tp")
        slopes = []
        for h in range(LOCAL_HEADS):
            s = jnp.float32(0.0)
            for d in range(TP):
                s = jnp.where(me == d, jnp.float32(2.0 ** (-8.0 * (LOCAL_HEADS * d + h + 1) / HEADS)), s)
            slopes.append(s)
        slope = jnp.where(iota((2 * BATCH, 1), 0) % 2 == 0, slopes[0], slopes[1])
        eye = one_hot(iota((BATCH, BATCH), 0) == iota((BATCH, BATCH), 1))
        hit = one_hot(iota((CACHE, BATCH), 0) == ws_ref[...])
        is_new = dot_nt(eye, hit)
        new_ref[...] = is_new
        allowed = one_hot(jnp.logical_or(kv_ref[...] > 0, is_new > 0.5))
        pos = dot(expand, kp_ref[...].astype(F32).astype(BF16))
        bias_ref[...] = jnp.where(dot(expand, allowed) > 0.5, slope * pos, -jnp.inf)
    else:
        abuf[...] = x_ref[...].reshape(BATCH, HIDDEN)

    wq_copy.wait()
    qkv = dot_nt(abuf[...], wq[...]) + bq[layer:layer + 1, :].astype(F32)
    qkv = qkv.astype(BF16).astype(F32)
    wide = jnp.concatenate([qkv, jnp.zeros((BATCH, 640 - QKV), F32)], axis=1)
    for i in range(5):
        t = jnp.transpose(wide[:, 128 * i:128 * (i + 1)])
        lo = 128 * i
        for h in range(LOCAL_HEADS):
            for part in range(2):
                src = h * 3 * HEAD + (part + 1) * HEAD
                dst = part * HD + h * HEAD
                a, b = max(lo, src), min(lo + 128, src + HEAD)
                if a < b:
                    kvt[dst + a - src:dst + b - src, :] = t[a - lo:b - lo, :]
    q_rows = jnp.concatenate([qkv[:, h * 3 * HEAD:h * 3 * HEAD + HEAD] for h in range(LOCAL_HEADS)], axis=1).astype(BF16)
    q_dup = dot(expand, q_rows).astype(BF16)
    col, n = iota((HD, GK), 0), iota((HD, GK), 1)
    tile = one_hot(functools.reduce(jnp.logical_or, [n == col + HD * j for j in range(GROUP)]))
    n = iota((BATCH, GK), 1)
    start = (iota((BATCH, GK), 0) % GROWS) * HEAD
    block = jnp.logical_and(n >= start, n < start + HEAD)
    for i in range(2):
        qbig[pl.ds(i * BATCH, BATCH), :] = jnp.where(block, dot(q_dup[i * BATCH:(i + 1) * BATCH], tile), 0.0).astype(BF16)

    scale = 1.0 / math.sqrt(HEAD)
    n16 = iota((GROWS, GK), 1)
    start16 = iota((GROWS, GK), 0) * HEAD
    diag = jnp.logical_and(n16 >= start16, n16 < start16 + HEAD)

    def rows16(g):
        return pl.ds(pl.multiple_of(g * GROWS, GROWS), GROWS)

    def update_and_score(g):
        k_in(g).wait()
        v_in(g).wait()
        cols = pltpu.roll(kvt[...], lax.rem(BATCH - g * GROUP, BATCH), 1)
        masks = new_ref[pl.ds(pl.multiple_of(g * GROUP, GROUP), GROUP), :]
        for j in range(GROUP):
            mask = masks[j:j + 1, :].astype(BF16) > 0
            for buf, lo in ((kbuf, 0), (vbuf, HD)):
                new = jnp.broadcast_to(cols[lo:lo + HD, j:j + 1], (HD, CACHE)).astype(BF16)
                old = buf[g, j * HD:(j + 1) * HD, :]
                buf[g, j * HD:(j + 1) * HD, :] = jnp.where(jnp.broadcast_to(mask, (HD, CACHE)), new, old)
        sbuf[rows16(g), :] = dot(qbig[rows16(g), :], kbuf[g])
        k_back(g).start()
        v_back(g).start()

    def soften(g):
        s = sbuf[rows16(g), :] * scale + bias_ref[rows16(g), :]
        e = jnp.exp(s - jnp.max(s, axis=-1, keepdims=True))
        pbuf[rows16(g), :] = (e / jnp.sum(e, axis=-1, keepdims=True)).astype(BF16)

    def mix(g):
        o = jnp.where(diag, dot_nt(pbuf[rows16(g), :], vbuf[g]), 0.0)
        w = 2 * HD
        ebuf[rows16(g), :] = sum(o[:, i * w:(i + 1) * w] for i in range(GK // w)).astype(BF16)

    def step(g, c):
        update_and_score(g)
        soften(g)
        mix(g)
        return c

    lax.fori_loop(0, NGROUP, step, 0)

    pair = one_hot(iota((BATCH, 2 * BATCH), 1) // 2 == iota((BATCH, 2 * BATCH), 0))
    o2 = dot(pair, ebuf[...]).astype(BF16)
    for copy in wo_copies:
        copy.wait()
    for c in range(NCHUNK):
        cs = slice(c * CHUNK, (c + 1) * CHUNK)
        part_ref[:, :, :, cs] = dot(o2, wo[:, cs]).reshape(4, 2, ROWS, CHUNK)

    def finish(g, c):
        k_back(g).wait()
        v_back(g).wait()
        return c

    lax.fori_loop(0, NGROUP, finish, 0)


def attention(layer, x, ln, w_qkv, b_qkv, w_out, k, v, small, prev):
    vmem, hbm = pl.BlockSpec(memory_space=pltpu.VMEM), pl.BlockSpec(memory_space=pl.ANY)
    cache = jax.ShapeDtypeStruct(k.shape, BF16)
    part = jax.ShapeDtypeStruct((4, 2, ROWS, HIDDEN), F32)
    if layer == 0:
        args = (x, *ln, w_qkv, b_qkv, w_out, k, v, *small)
        in_specs = [vmem, vmem, vmem, hbm, vmem, hbm, hbm, hbm, vmem, vmem, vmem]
        outs = (part, cache, cache, jax.ShapeDtypeStruct((2 * BATCH, CACHE), F32), jax.ShapeDtypeStruct((BATCH, CACHE), F32))
        out_specs = (vmem, hbm, hbm, vmem, vmem)
        aliases = {}
    else:
        args = (x, w_qkv, b_qkv, w_out, k, v, *small, *prev)
        in_specs = [vmem, hbm, vmem, hbm, hbm, hbm, vmem, vmem, hbm, hbm]
        outs = (part, cache, cache)
        out_specs = (vmem, hbm, hbm)
        aliases = {8: 1, 9: 2}
    return pl.pallas_call(
        functools.partial(att_kernel, layer),
        out_shape=outs, in_specs=in_specs, out_specs=out_specs,
        input_output_aliases=aliases,
        scratch_shapes=[
            pltpu.VMEM((NGROUP, GK, CACHE), BF16),
            pltpu.VMEM((NGROUP, GK, CACHE), BF16),
            pltpu.VMEM((QKV, HIDDEN), BF16),
            pltpu.VMEM((2 * HD, HIDDEN), BF16),
            pltpu.VMEM((BATCH, HIDDEN), BF16),
            pltpu.VMEM((2 * BATCH, GK), BF16),
            pltpu.VMEM((2 * HD, BATCH), F32),
            pltpu.VMEM((2 * BATCH, 2 * HD), BF16),
            pltpu.VMEM((2 * BATCH, CACHE), F32),
            pltpu.VMEM((2 * BATCH, CACHE), BF16),
            pltpu.SemaphoreType.DMA((2, NGROUP)),
            pltpu.SemaphoreType.DMA((2, NGROUP)),
            pltpu.SemaphoreType.DMA((3,)),
        ],
        compiler_params=pltpu.CompilerParams(vmem_limit_bytes=48 * 1024 * 1024),
        cost_estimate=pl.CostEstimate(flops=400_000_000, bytes_accessed=53_000_000, transcendentals=65536),
        name=f"att{layer}",
    )(*args)


def comm_kernel(layer, part_in, x_ref, lng, lnb, bo, wu_hbm, bu, wd_hbm, bd, *refs):
    last = layer == 1
    if last:
        (x_out,) = refs[:1]
        refs = refs[1:]
    else:
        a_out, x_out = refs[:2]
        refs = refs[2:]
    (part, pair_buf, send_buf, recv_buf, own, gathered, hidden, gelu, wu, wd,
     wsem, d_send, d_recv, r_send, r_recv, g_send, g_recv) = refs
    me = lax.axis_index("tp")
    chip, core = me // 2, me % 2
    other = 1 - core
    cx, cy = chip % 2, chip // 2
    chips = [2 * (1 - cy) + (1 - cx), 2 * cy + (1 - cx), 2 * (1 - cy) + cx]
    wu_copy = pltpu.make_async_copy(wu_hbm.at[layer], wu, wsem.at[0])
    wd_copy = pltpu.make_async_copy(wd_hbm.at[layer], wd, wsem.at[1])
    wu_copy.start()
    wd_copy.start()

    barrier = pltpu.get_barrier_semaphore()
    for k in range(1, TP):
        pl.semaphore_signal(barrier, inc=1, device_id={"tp": lax.rem(me + k, TP)}, device_id_type=MESH)
    pl.semaphore_wait(barrier, TP - 1)

    def pair_copy(src, c):
        cs = pl.ds(c * CHUNK, CHUNK)
        return pltpu.make_async_remote_copy(
            src.at[:, other, :, cs], pair_buf.at[:, :, cs], d_send.at[c], d_recv.at[c],
            device_id={"tp": 2 * chip + other}, device_id_type=MESH)

    def reduce_copy(k, c):
        cs = pl.ds(c * CHUNK, CHUNK)
        return pltpu.make_async_remote_copy(
            send_buf.at[k, :, cs], recv_buf.at[k, :, cs], r_send.at[c, k], r_recv.at[c, k],
            device_id={"tp": 2 * chips[k] + core}, device_id_type=MESH)

    def gather_copy(k, c):
        cs = pl.ds(c * CHUNK, CHUNK)
        return pltpu.make_async_remote_copy(
            own.at[:, cs], gathered.at[me, :, cs], g_send.at[c, k - 1], g_recv.at[c, k - 1],
            device_id={"tp": lax.rem(me + k, TP)}, device_id_type=MESH)

    def reduce_scatter(src):
        for c in range(NCHUNK):
            cs = slice(c * CHUNK, (c + 1) * CHUNK)
            pair_copy(src, c).wait_recv()
            for k in range(3):
                send_buf[k, :, cs] = src[chips[k], core, :, cs] + pair_buf[chips[k], :, cs]
                reduce_copy(k, c).start()
        total = src[chip, core] + pair_buf[chip]
        for c in range(NCHUNK):
            for k in range(3):
                reduce_copy(k, c).wait_recv()
        for k in range(3):
            total = total + recv_buf[k]
        for c in range(NCHUNK):
            pair_copy(src, c).wait_send()
            for k in range(3):
                reduce_copy(k, c).wait_send()
        return total

    def start_gather():
        gathered[me] = own[...]
        for c in range(NCHUNK):
            for k in range(1, TP):
                gather_copy(k, c).start()

    def wait_gather(c):
        for k in range(1, TP):
            gather_copy(k, c).wait_recv()

    def end_gather():
        for c in range(NCHUNK):
            for k in range(1, TP):
                gather_copy(k, c).wait_send()

    for c in range(NCHUNK):
        pair_copy(part_in, c).start()
    total = reduce_scatter(part_in)
    if layer == 0:
        x_own = x_ref[pl.ds(pl.multiple_of(me * ROWS, ROWS), ROWS), :]
    else:
        x_own = x_ref[...]
    x_mid = (x_own.astype(F32) + total + bo[layer:layer + 1, :].astype(F32)).astype(BF16)
    own[...] = layer_norm(x_mid.astype(F32), lng[layer, 1:2, :], lnb[layer, 1:2, :])
    start_gather()
    wu_copy.wait()
    for c in range(NCHUNK):
        wait_gather(c)
        cs = slice(c * CHUNK, (c + 1) * CHUNK)
        up = dot(gathered[:, :, cs].reshape(BATCH, CHUNK), wu[cs, :])
        hidden[...] = up if c == 0 else hidden[...] + up
    act = jax.nn.gelu(hidden[...] + bu[layer:layer + 1, :].astype(F32), approximate=True)
    gelu[...] = act.astype(BF16)
    end_gather()
    wd_copy.wait()
    for c in range(NCHUNK):
        cs = slice(c * CHUNK, (c + 1) * CHUNK)
        part[:, :, :, cs] = dot(gelu[...], wd[:, cs]).reshape(4, 2, ROWS, CHUNK)
        pair_copy(part, c).start()
    total = reduce_scatter(part)
    x_new = (x_mid.astype(F32) + total + bd[layer:layer + 1, :].astype(F32)).astype(BF16)
    if last:
        own[...] = x_new
    else:
        x_out[...] = x_new
        own[...] = layer_norm(x_new.astype(F32), lng[layer + 1, 0:1, :], lnb[layer + 1, 0:1, :])
    start_gather()
    for c in range(NCHUNK):
        wait_gather(c)
    if last:
        x_out[...] = gathered[...]
    else:
        a_out[...] = gathered[...]
    end_gather()


def communicate(layer, part, x, ln, b_out, w_up, b_up, w_down, b_down):
    vmem, hbm = pl.BlockSpec(memory_space=pltpu.VMEM), pl.BlockSpec(memory_space=pl.ANY)
    full = jax.ShapeDtypeStruct((TP, ROWS, HIDDEN), BF16)
    outs = (full, jax.ShapeDtypeStruct((ROWS, HIDDEN), BF16)) if layer == 0 else (full,)
    return pl.pallas_call(
        functools.partial(comm_kernel, layer),
        out_shape=outs,
        in_specs=[vmem, vmem, vmem, vmem, vmem, hbm, vmem, hbm, vmem],
        out_specs=(vmem,) * len(outs),
        scratch_shapes=[
            pltpu.VMEM((4, 2, ROWS, HIDDEN), F32),
            pltpu.VMEM((4, ROWS, HIDDEN), F32),
            pltpu.VMEM((3, ROWS, HIDDEN), F32),
            pltpu.VMEM((3, ROWS, HIDDEN), F32),
            pltpu.VMEM((ROWS, HIDDEN), BF16),
            pltpu.VMEM((TP, ROWS, HIDDEN), BF16),
            pltpu.VMEM((BATCH, FF), F32),
            pltpu.VMEM((BATCH, FF), BF16),
            pltpu.VMEM((HIDDEN, FF), BF16),
            pltpu.VMEM((FF, HIDDEN), BF16),
            pltpu.SemaphoreType.DMA((2,)),
            pltpu.SemaphoreType.DMA((NCHUNK,)),
            pltpu.SemaphoreType.DMA((NCHUNK,)),
            pltpu.SemaphoreType.DMA((NCHUNK, 3)),
            pltpu.SemaphoreType.DMA((NCHUNK, 3)),
            pltpu.SemaphoreType.DMA((NCHUNK, TP - 1)),
            pltpu.SemaphoreType.DMA((NCHUNK, TP - 1)),
        ],
        compiler_params=pltpu.CompilerParams(collective_id=layer, has_side_effects=True, vmem_limit_bytes=24 * 1024 * 1024),
        cost_estimate=pl.CostEstimate(flops=650_000_000, bytes_accessed=6_000_000, transcendentals=98304),
        name=f"comm{layer}",
    )(part, x, *ln, b_out, w_up, b_up, w_down, b_down)


def solution(mesh):
    def device_step(hidden, ln_gain, ln_shift, w_qkv, b_qkv, w_out, b_out, w_up, b_up, w_down, b_down, k_cache, v_cache, write_slot, key_pos, key_valid):
        def stacked(cache):
            return jnp.transpose(cache, (0, 1, 3, 4, 2)).reshape(2, NGROUP, GK, CACHE)

        def unstacked(cache):
            return jnp.transpose(cache.reshape(2, BATCH, LOCAL_HEADS, HEAD, CACHE), (0, 1, 4, 2, 3))

        k, v = stacked(k_cache), stacked(v_cache)
        wq = jnp.transpose(w_qkv, (0, 2, 1))
        x = hidden[:, 0, :]
        ln = (ln_gain, ln_shift)
        small = (write_slot.reshape(1, BATCH), key_pos, key_valid)
        part, k_new, v_new, bias, is_new = attention(0, x, ln, wq, b_qkv, w_out, k, v, small, ())
        a_next, x_own = communicate(0, part, x, ln, b_out, w_up, b_up, w_down, b_down)
        part, k_new, v_new = attention(1, a_next, (), wq, b_qkv, w_out, k, v, (bias, is_new), (k_new, v_new))
        (x_last,) = communicate(1, part, x_own, ln, b_out, w_up, b_up, w_down, b_down)
        return x_last.reshape(BATCH, 1, HIDDEN), unstacked(k_new), unstacked(v_new)

    cache_spec = P(None, 'dp', None, 'tp', None)
    in_specs = (P('dp', None, None), P(), P(), P(None, None, 'tp'), P(None, 'tp'), P(None, 'tp', None), P(), P(None, None, 'tp'), P(None, 'tp'), P(None, 'tp', None), P(), cache_spec, cache_spec, P('dp'), P('dp', None), P('dp', None))
    out_specs = (P('dp', None, None), cache_spec, cache_spec)
    return jax.shard_map(device_step, mesh=mesh, in_specs=in_specs, out_specs=out_specs, check_vma=False)
```

time: 285 us -> 113 us (0.40)
  waiting for transfers between devices: 136 us -> 0 us
  Pallas kernels: 0 us -> 104 us
  other arithmetic: 88.5 us -> 0 us
  matrix products: 43.8 us -> 0 us
  between operations: 14 us -> 0.8 us
  local copies, waits for them, and re-layouts: 1.1 us -> 7.6 us
    psum x4 -> x0, waiting for transfers between devices: 136 us -> none  [the longest x2 69.8 us: device_step(): proj_sum = lax.psum(proj_part, 'tp')]
    pallas_call x0 -> x4, Pallas kernels: none -> 104 us  [the longest x2 64.4 us: communicate(): pl.pallas_call(functools.partial(comm_kernel, layer), out_shape=outs, in_...]
    dot_general x10 -> x0, matrix products: 43.8 us -> none  [the longest x2 14.1 us: device_step(): jnp.einsum('bht,bthd->bhd', attn_probs, v_all, preferred_element_type=jnp...]
    another operation x2 -> x0, other arithmetic: 41.3 us -> none  [device_step(): return (x_cur[:, None, :], jnp.stack(k_list), jnp.stack(v_list))]
    select_n x1 -> x0, other arithmetic: 33.7 us -> none  [device_step(): v_all = jnp.where(new_mask, qkv_out[:, None, :, 2, :], v_cache[layer_idx])]
    unnamed x10 -> x35, local copies, waits for them, and re-layouts: 0.03 us -> 7.6 us
    reduce_sum x8 -> x0, other arithmetic: 7.15 us -> none  [the longest x4 5.13 us: layer_norm(): mean_val = jnp.mean(x_f32, axis=-1, keepdims=True)]
  transfers between devices with their start and end apart: 4 -> 0, of which waited for: 4 -> 0; matrix products, arithmetic and copies ran while one was open for 15% -> 0% of each run, Pallas kernels for 0% -> 0%
where the time goes in v1:
time: 113 us
  Pallas kernels  104 us (92%)
  local copies, waits for them, and re-layouts  7.6 us (7%)
    pallas_call x2, Pallas kernels, communicate(): pl.pallas_call(functools.partial(comm_kernel, layer), out_shape=outs, in_...  64.4 us
    pallas_call x2, Pallas kernels, attention(): pl.pallas_call(functools.partial(att_kernel, layer), out_shape=outs, in_s...  40 us
    unnamed x35, local copies, waits for them, and re-layouts  7.6 us

profile of v1, /device:TPU:0, one launch (start us, length us, event | category | flops | bytes accessed | tf_op | source)
XLA Modules:
  0.0 112.8 jit_solution(8755279283336870169)
XLA Ops:
  0.6 0.0 copy-start.2
  0.6 1.3 %copy-done.2 = bf16[2,192,1536]{2,1,0:T(8,128)(2,1)S(1)} copy-done((bf16[2,192,1536]{2,1,0:T(8,128)(2,1)S(1)}, bf16[2,192,1536]{2,1,0:T(8,128)(2,1)}, u32[]{:S(2)}) %copy-start.2) | copy-done | bytes 1179672
  1.9 0.0 copy-start.4
  1.9 1.0 copy-done.4
  2.9 0.0 copy-start.5
  2.9 0.9 copy-done.5
  3.8 0.0 copy-start.6
  3.8 0.9 copy-done.6
  4.7 0.0 copy-start.7
  4.7 0.7 copy-done.7
  5.4 0.7 copy-done.9
  6.1 0.7 copy-done.14
  6.8 0.7 copy-done.16
  7.5 0.0 copy-start.11
  7.5 0.0 copy-start.12
  7.5 0.0 copy-start.13
  7.5 0.0 copy-start.3
  7.5 0.0 copy-start.15
  7.5 20.5 %att0.1 = (f32[4,2,16,1536]{3,2,1,0:T(8,128)S(1)}, bf16[2,16,1536,256]{3,2,1,0:T(8,128)(2,1)}, bf16[2,16,1536,256]{3,2,1,0:T(8,128)(2,1)}, f32[256,256]{1,0:T(8,128)S(1)}, f32[128,256]{1,0:T(8,128)S(1)}) custom-call(bf16[128,1536]{1,0:T(8,128)(2,1)S(1)} %bitcast.16, bf16[2,2,1536]{2,1,0:T(2,128)(2,1)S(1)} %copy-done.7, bf16[2,2,1536]{2,1,0:T(2,128)(2,1)S(1)} %copy-done.9, ...), custom_call_target="tpu_custom_call" | custom-call | flops 400000000 | bytes 53000000 | tf_op jit(solution)/shard_map/att0/pallas_call | solution.py:212
  28.0 0.0 copy-done
  28.0 0.0 copy-done.1
  28.0 0.0 copy-done.8
  28.0 0.0 copy-done.10
  28.0 0.0 copy-done.11
  28.0 0.0 copy-done.12
  28.1 0.0 copy-done.13
  28.1 33.5 %comm0.1 = (bf16[8,16,1536]{2,1,0:T(8,128)(2,1)S(1)}, bf16[16,1536]{1,0:T(8,128)(2,1)S(1)}) custom-call(f32[4,2,16,1536]{3,2,1,0:T(8,128)S(1)} %get-tuple-element.13.part_in, bf16[128,1536]{1,0:T(8,128)(2,1)S(1)} %bitcast.17, bf16[2,2,1536]{2,1,0:T(2,128)(2,1)S(1)} %copy-done.8, bf16[2,2,1536]{2,1,0:T(2,128)(2,1)S(1)} %copy-done.10, ...), custom_call_target="tpu_custom_call" | custom-call | flops 650000000 | bytes 6000000 | tf_op jit(solution)/shard_map/comm0/pallas_call | solution.py:359
  61.6 0.0 copy-done.3
  61.6 0.0 copy-done.15
  61.6 19.5 %att1.1 = (f32[4,2,16,1536]{3,2,1,0:T(8,128)S(1)}, bf16[2,16,1536,256]{3,2,1,0:T(8,128)(2,1)}, bf16[2,16,1536,256]{3,2,1,0:T(8,128)(2,1)}) custom-call(bf16[8,16,1536]{2,1,0:T(8,128)(2,1)S(1)} %get-tuple-element.14.refs_0_, bf16[2,576,1536]{2,1,0:T(8,128)(2,1)} %bitcast.27, ...), custom_call_target="tpu_custom_call", output_to_operand_aliasing={{1}: (8, {}), {2}: (9, {})} | custom-call | flops 400000000 | bytes 53000000 | tf_op jit(solution)/shard_map/att1/pallas_call | solution.py:212
  81.2 30.9 %comm1.1 = bf16[8,16,1536]{2,1,0:T(8,128)(2,1)S(1)} custom-call(f32[4,2,16,1536]{3,2,1,0:T(8,128)S(1)} %get-tuple-element.19.part_in, bf16[16,1536]{1,0:T(8,128)(2,1)S(1)} %get-tuple-element.20.x_ref, bf16[2,2,1536]{2,1,0:T(2,128)(2,1)S(1)} %copy-done.8, bf16[2,2,1536]{2,1,0:T(2,128)(2,1)S(1)} %copy-done.10, bf16[2,1536]{1,0:T(2,128)(2,1)S(1)} %copy-done.11, ...), custom_call_target="tpu_custom_call" | custom-call | flops 650000000 | bytes 6000000 | tf_op jit(solution)/shard_map/comm1/pallas_call | solution.py:359
  112.1 0.7 copy.24
  (7 shorter events, 0.0 us)
Async XLA Ops:
  0.6 1.3 %copy-start.2 = (bf16[2,192,1536]{2,1,0:T(8,128)(2,1)S(1)}, bf16[2,192,1536]{2,1,0:T(8,128)(2,1)}, u32[]{:S(2)}) copy-start(bf16[2,192,1536]{2,1,0:T(8,128)(2,1)} %refs_3_.1) | copy-start | bytes 3538948
  1.9 1.0 copy-start.4
  2.9 0.9 copy-start.5
  3.8 0.9 copy-start.6
  4.7 0.7 copy-start.7
  5.4 0.7 copy-start.9
  6.1 0.7 copy-start.14
  6.8 0.7 copy-start.16
  7.5 20.5 %copy-start = (bf16[2,1536,768]{2,1,0:T(8,128)(2,1)S(1)}, bf16[2,1536,768]{2,1,0:T(8,128)(2,1)}, u32[]{:S(2)}) copy-start(bf16[2,1536,768]{2,1,0:T(8,128)(2,1)} %wu_hbm.3) | copy-start | bytes 14155780
  7.5 20.5 %copy-start.1 = (bf16[2,768,1536]{2,1,0:T(8,128)(2,1)S(1)}, bf16[2,768,1536]{2,1,0:T(8,128)(2,1)}, u32[]{:S(2)}) copy-start(bf16[2,768,1536]{2,1,0:T(8,128)(2,1)} %wd_hbm.3) | copy-start | bytes 14155780
  7.5 20.5 %copy-start.8 = (bf16[2,2,1536]{2,1,0:T(2,128)(2,1)S(1)}, bf16[2,2,1536]{2,1,0:T(2,128)(2,1)}, u32[]{:S(2)}) copy-start(bf16[2,2,1536]{2,1,0:T(2,128)(2,1)} %lng.3) | copy-start | bytes 36868
  7.5 20.6 %copy-start.10 = (bf16[2,2,1536]{2,1,0:T(2,128)(2,1)S(1)}, bf16[2,2,1536]{2,1,0:T(2,128)(2,1)}, u32[]{:S(2)}) copy-start(bf16[2,2,1536]{2,1,0:T(2,128)(2,1)} %lnb.3) | copy-start | bytes 36868
  7.5 20.6 %copy-start.11 = (bf16[2,1536]{1,0:T(2,128)(2,1)S(1)}, bf16[2,1536]{1,0:T(2,128)(2,1)}, u32[]{:S(2)}) copy-start(bf16[2,1536]{1,0:T(2,128)(2,1)} %bo.3) | copy-start | bytes 18436
  7.5 20.6 %copy-start.12 = (bf16[2,1536]{1,0:T(2,128)(2,1)S(1)}, bf16[2,1536]{1,0:T(2,128)(2,1)}, u32[]{:S(2)}) copy-start(bf16[2,1536]{1,0:T(2,128)(2,1)} %bd.3) | copy-start | bytes 18436
  7.5 20.6 %copy-start.13 = (bf16[2,768]{1,0:T(2,128)(2,1)S(1)}, bf16[2,768]{1,0:T(2,128)(2,1)}, u32[]{:S(2)}) copy-start(bf16[2,768]{1,0:T(2,128)(2,1)} %bu.3) | copy-start | bytes 9220
  7.5 54.1 %copy-start.3 = (bf16[2,192,1536]{2,1,0:T(8,128)(2,1)S(1)}, bf16[2,192,1536]{2,1,0:T(8,128)(2,1)}, u32[]{:S(2)}) copy-start(bf16[2,192,1536]{2,1,0:T(8,128)(2,1)} %refs_3_.1) | copy-start | bytes 3538948
  7.5 54.1 %copy-start.15 = (bf16[2,576]{1,0:T(2,128)(2,1)S(1)}, bf16[2,576]{1,0:T(2,128)(2,1)}, u32[]{:S(2)}) copy-start(bf16[2,576]{1,0:T(2,128)(2,1)} %refs_2_.3) | copy-start | bytes 6916
